TPU v7x, 512 devices: a whole 4x4x16 slice. The times are simulated.
512 devices in a mesh: group: 4 (over z_hi, core), gx: 32 (over z_lo, y), gy: 4 (over x).
Axes of the slice: x: 4, y: 4, z: 16 (z_hi: 2, z_lo: 8; z = z_hi * 8 + z_lo), core: 2. Of those that a mesh axis runs over, the one named last changes fastest.
Arguments:
- parent_mass: float32 [512, 512, 512], P('gx', ('group', 'gy')), may hold values from -6 to 6
- fine_mass: float32 [512, 128, 128], P('gx', ('group', 'gy')), may hold values from -6 to 6
- offsets: int32 [3], replicated, may hold values from 0 to 511
Outputs:
- parent_potential: float32 [512, 512, 512], P('gx', ('group', 'gy'))
- fine_potential: float32 [512, 128, 128], P('gx', ('group', 'gy'))
All inputs are finite; a program needn't handle non-finite values.
Results may differ from a plain program's by a relative error of at most 0.0003.
Values sent between devices are 32-bit elements; how exact they have to be, the bound alone decides.
No kernel may reach another device: no remote copies, remote signals or barrier semaphores. Data moves between devices by JAX's collectives and lax.ppermute only.
A program may use at most 128 MiB of HBM per device.

v0:
```python
import math
import jax
import jax.numpy as jnp
from jax import lax
from jax.sharding import PartitionSpec as P

NP = 512
CYCLES = 2
LEVELS = 3
SWEEPS = 2
COARSE_SWEEPS = 4
OMEGA = 6.0 / 7.0
HIGH = lax.Precision.HIGHEST


def extended(shard, sides, width):
    edges = {}
    for axis, dim in sides:
        size, length = (lax.axis_size(axis), shard.shape[dim])
        up = [(i, (i + 1) % size) for i in range(size - 1)]
        last = lax.slice_in_dim(shard, length - width, length, axis=dim)
        initial = lax.slice_in_dim(shard, 0, width, axis=dim)
        edges[dim] = (
            lax.ppermute(last, axis, up),
            lax.ppermute(initial, axis, [(b, a) for a, b in up]),
        )
    done = []
    for _, dim in sides:
        low, high = edges[dim]
        around = [(width, width) if d in done else (0, 0) for d in range(shard.ndim)]
        shard = jnp.concatenate([jnp.pad(low, around), shard, jnp.pad(high, around)], axis=dim)
        done.append(dim)
    return shard


def cas_table(wave, places, length):
    phase = wave[:, None] * places[None, :] % length
    angle = phase.astype(jnp.float32) * (2.0 * math.pi / length)
    return jnp.cos(angle) + jnp.sin(angle)


def eigen_of(wave, length):
    sine = jnp.sin(wave.astype(jnp.float32) * (math.pi / length))
    return 4.0 * sine * sine


def green(wave_a, wave_b, wave_c):
    lam = (
        eigen_of(wave_a, NP)[:, None, None]
        + eigen_of(wave_b, NP)[None, :, None]
        + eigen_of(wave_c, NP)[None, None, :]
    )
    inverse = jnp.where(lam > 0, 1.0 / jnp.where(lam > 0, lam, 1.0), 0.0)
    return inverse * (1.0 / float(NP**3))


def last_axis(block, table):
    return jnp.einsum("abj,kj->abk", block, table, precision=HIGH)


def middle_axis(block, table):
    return jnp.einsum("ajc,kj->akc", block, table, precision=HIGH)


def first_axis(block, table):
    product = jnp.dot(table, block.reshape(block.shape[0], -1), precision=HIGH)
    return product.reshape((table.shape[0],) + block.shape[1:])


def coarsen(block):
    a, b, c = block.shape
    return block.reshape(a // 2, 2, b // 2, 2, c // 2, 2).sum(axis=(1, 3, 5))


def refine(block):
    return jnp.repeat(jnp.repeat(jnp.repeat(block, 2, axis=0), 2, axis=1), 2, axis=2)


def stencil(field, padded):
    beside = padded[2:, 1:-1, 1:-1] + padded[:-2, 1:-1, 1:-1]
    beside = beside + padded[1:-1, 2:, 1:-1] + padded[1:-1, :-2, 1:-1]
    beside = beside + padded[1:-1, 1:-1, 2:] + padded[1:-1, 1:-1, :-2]
    return 6.0 * field - beside


def operate(field, edge, flags):
    padded = extended(field, (("gx", 0), (("group", "gy"), 1)), 1)
    if edge:
        padded = padded.at[0, 1:-1].set(jnp.where(flags[0], field[0], padded[0, 1:-1]))
        padded = padded.at[-1, 1:-1].set(jnp.where(flags[1], field[-1], padded[-1, 1:-1]))
        padded = padded.at[1:-1, 0].set(jnp.where(flags[2], field[:, 0], padded[1:-1, 0]))
        padded = padded.at[1:-1, -1].set(jnp.where(flags[3], field[:, -1], padded[1:-1, -1]))
        padded = jnp.pad(padded, ((0, 0), (0, 0), (1, 1)), mode="edge")
    else:
        padded = jnp.pad(padded, ((0, 0), (0, 0), (1, 1)))
    return stencil(field, padded)


def smooth(corr, resid, sweeps, flags):
    for turn in range(sweeps):
        if corr is None:
            corr = OMEGA / 6.0 * resid
        else:
            corr = corr + OMEGA / 6.0 * (resid - operate(corr, False, flags))
    return corr


def coarsest(resid, flags):
    return smooth(None, resid, COARSE_SWEEPS, flags)


def cycle(corr, resid, level, flags, index_x, index_y):
    if level == LEVELS - 1:
        return coarsest(resid, flags)
    corr = smooth(corr, resid, SWEEPS, flags)
    lower = 0.5 * coarsen(resid - operate(corr, False, flags))
    below = cycle(None, lower, level + 1, flags, index_x, index_y)
    corr = corr + refine(below)
    return smooth(corr, resid, SWEEPS, flags)


def local(parent_mass, fine_mass, offsets):
    count_x = lax.axis_size("gx")
    count_y = lax.axis_size(("group", "gy"))
    index_x = lax.axis_index("gx")
    index_y = lax.axis_index(("group", "gy"))
    wave = jnp.arange(NP, dtype=jnp.int32)
    full = cas_table(wave, wave, NP)
    rest = coarsen(fine_mass)
    span_x = rest.shape[0] * count_x
    span_y = rest.shape[1] * count_y
    x_table = cas_table(wave, offsets[0] + jnp.arange(span_x, dtype=jnp.int32), NP)
    y_table = cas_table(wave, offsets[1] + jnp.arange(span_y, dtype=jnp.int32), NP)
    z_table = cas_table(wave, offsets[2] + jnp.arange(rest.shape[2], dtype=jnp.int32), NP)
    dense = last_axis(parent_mass, full)
    light = last_axis(rest, z_table)
    dense, light = (
        lax.all_to_all(dense, "gx", split_axis=2, concat_axis=0, tiled=True),
        lax.all_to_all(light, "gx", split_axis=2, concat_axis=0, tiled=True),
    )
    dense = first_axis(dense, full)
    light = first_axis(light, x_table)
    dense, light = (
        lax.all_to_all(dense, ("group", "gy"), split_axis=0, concat_axis=1, tiled=True),
        lax.all_to_all(light, ("group", "gy"), split_axis=0, concat_axis=1, tiled=True),
    )
    spectrum = middle_axis(dense, full) + middle_axis(light, y_table)
    width_a = spectrum.shape[0]
    width_c = spectrum.shape[2]
    spectrum = spectrum * green(
        index_y * width_a + jnp.arange(width_a, dtype=jnp.int32),
        wave,
        index_x * width_c + jnp.arange(width_c, dtype=jnp.int32),
    )
    whole = middle_axis(spectrum, full)
    near = middle_axis(spectrum, y_table.T)
    whole, near = (
        lax.all_to_all(whole, ("group", "gy"), split_axis=1, concat_axis=0, tiled=True),
        lax.all_to_all(near, ("group", "gy"), split_axis=1, concat_axis=0, tiled=True),
    )
    whole = first_axis(whole, full)
    near = first_axis(near, x_table.T)
    whole, near = (
        lax.all_to_all(whole, "gx", split_axis=0, concat_axis=2, tiled=True),
        lax.all_to_all(near, "gx", split_axis=0, concat_axis=2, tiled=True),
    )
    potential = last_axis(whole, full)
    footprint = last_axis(near, z_table.T)
    flags = (index_x == 0, index_x == count_x - 1, index_y == 0, index_y == count_y - 1)
    start = refine(footprint)
    resid = 2.0 * fine_mass - operate(start, True, flags)
    corr = None
    for turn in range(CYCLES):
        corr = cycle(corr, resid, 0, flags, index_x, index_y)
    return (potential, start + corr)


def solution(mesh):
    return jax.shard_map(
        local,
        mesh=mesh,
        in_specs=(P("gx", ("group", "gy"), None), P("gx", ("group", "gy"), None), P()),
        out_specs=(P("gx", ("group", "gy"), None), P("gx", ("group", "gy"), None)),
        check_vma=False,
    )
```

profile of v0, /device:TPU:135, one launch (start us, length us, event | category | flops | bytes accessed | tf_op | source)
XLA Modules:
  0.0 1045.0 jit_solution(9459610186346306558)
XLA Ops:
  64.1 37.1 %all-to-all-done = f32[32,1,8192]{2,1,0:T(1,128)S(1)} async-done(((f32[32,1,8192]{2,1,0:T(1,128)}), f32[32,1,8192]{2,1,0:T(1,128)S(1)}, u32[]{:S(2)}, u32[]{:S(2)}) %all-to-all-start) | async-done | bytes 1048608 | tf_op jit(solution)/shard_map/all_to_all | solution.py:138
  148.6 14.7 %all-to-all-start.1 = ((f32[16,1,16384]{2,1,0:T(1,128)}), f32[16,1,16384]{2,1,0:T(1,128)S(1)}, u32[]{:S(2)}, u32[]{:S(2)}) async-start(f32[16,1,16384]{2,1,0:T(1,128)} %reshape.357), calls=%async_computation.1 | async-start | bytes 2097152 | tf_op jit(solution)/shard_map/all_to_all | solution.py:144
  167.2 50.5 %all-to-all-done.1 = f32[16,1,16384]{2,1,0:T(1,128)S(1)} async-done(((f32[16,1,16384]{2,1,0:T(1,128)}), f32[16,1,16384]{2,1,0:T(1,128)S(1)}, u32[]{:S(2)}, u32[]{:S(2)}) %all-to-all-start.1) | async-done | bytes 1048608 | tf_op jit(solution)/shard_map/all_to_all | solution.py:144
  244.9 18.9 %all_to_all.132 = f32[16,1,2048]{2,1,0:T(1,128)S(1)} all-to-all(f32[16,1,2048]{2,1,0:T(1,128)S(1)} %reshape.367), channel_id=1, replica_groups=mesh['group'=4,'gx'=32,'gy'=4] {'group','gy'}, dimensions={0} | all-to-all | bytes 262144 | tf_op jit(solution)/shard_map/all_to_all | solution.py:159
  321.5 14.5 %collective-permute-start.7 = (f32[16,1,128]{2,1,0:T(1,128)S(1)}, f32[16,1,128]{2,1,0:T(1,128)S(1)}, u32[]{:S(2)}, u32[]{:S(2)}) collective-permute-start(f32[16,1,128]{2,1,0:T(1,128)S(1)} %get-tuple-element.96), channel_id=1, source_target_pairs={{0,1},{1,2},{2,3},{3,128},{128,129},{129,130},{130,131},{131,256},... | collective-permute-start | bytes 24584 | tf_op jit(solution)/shard_map/ppermute | solution.py:24
  352.9 14.5 %collective-permute-start.11 = (f32[16,1,128]{2,1,0:T(1,128)S(1)}, f32[16,1,128]{2,1,0:T(1,128)S(1)}, u32[]{:S(2)}, u32[]{:S(2)}) collective-permute-start(f32[16,1,128]{2,1,0:T(1,128)S(1)} %get-tuple-element.92), channel_id=1, source_target_pairs={{0,1},{1,2},{2,3},{3,128},{128,129},{129,130},{130,131},{131,256},... | collective-permute-start | bytes 24584 | tf_op jit(solution)/shard_map/ppermute | solution.py:24
  387.5 14.5 %collective-permute-start.15 = (f32[8,1,64]{2,1,0:T(1,128)S(1)}, f32[8,1,64]{2,1,0:T(1,128)S(1)}, u32[]{:S(2)}, u32[]{:S(2)}) collective-permute-start(f32[8,1,64]{2,1,0:T(1,128)S(1)} %get-tuple-element.132), channel_id=1, source_target_pairs={{0,1},{1,2},{2,3},{3,128},{128,129},{129,130},{130,131},{131,256},... | collective-permute-start | bytes 6152 | tf_op jit(solution)/shard_map/ppermute | solution.py:24
  413.7 14.5 %collective-permute-start.19 = (f32[8,1,64]{2,1,0:T(1,128)S(1)}, f32[8,1,64]{2,1,0:T(1,128)S(1)}, u32[]{:S(2)}, u32[]{:S(2)}) collective-permute-start(f32[8,1,64]{2,1,0:T(1,128)S(1)} %get-tuple-element.128), channel_id=1, source_target_pairs={{0,1},{1,2},{2,3},{3,128},{128,129},{129,130},{130,131},{131,256},... | collective-permute-start | bytes 6152 | tf_op jit(solution)/shard_map/ppermute | solution.py:24
  440.6 14.5 %collective-permute-start.23 = (f32[4,1,32]{2,0,1:T(4,128)S(1)}, f32[4,1,32]{2,0,1:T(4,128)S(1)}, u32[]{:S(2)}, u32[]{:S(2)}) collective-permute-start(f32[4,1,32]{2,0,1:T(4,128)S(1)} %get-tuple-element.156), channel_id=1, source_target_pairs={{0,1},{1,2},{2,3},{3,128},{128,129},{129,130},{130,131},{131,256},... | collective-permute-start | bytes 1544 | tf_op jit(solution)/shard_map/ppermute | solution.py:24
  466.7 14.5 %collective-permute-start.27 = (f32[4,1,32]{2,0,1:T(4,128)S(1)}, f32[4,1,32]{2,0,1:T(4,128)S(1)}, u32[]{:S(2)}, u32[]{:S(2)}) collective-permute-start(f32[4,1,32]{2,0,1:T(4,128)S(1)} %get-tuple-element.152), channel_id=1, source_target_pairs={{0,1},{1,2},{2,3},{3,128},{128,129},{129,130},{130,131},{131,256},... | collective-permute-start | bytes 1544 | tf_op jit(solution)/shard_map/ppermute | solution.py:24
  492.9 14.5 %collective-permute-start.31 = (f32[4,1,32]{2,0,1:T(4,128)S(1)}, f32[4,1,32]{2,0,1:T(4,128)S(1)}, u32[]{:S(2)}, u32[]{:S(2)}) collective-permute-start(f32[4,1,32]{2,0,1:T(4,128)S(1)} %get-tuple-element.148), channel_id=1, source_target_pairs={{0,1},{1,2},{2,3},{3,128},{128,129},{129,130},{130,131},{131,256},... | collective-permute-start | bytes 1544 | tf_op jit(solution)/shard_map/ppermute | solution.py:24
  519.3 14.5 %collective-permute-start.35 = (f32[8,1,64]{2,1,0:T(1,128)S(1)}, f32[8,1,64]{2,1,0:T(1,128)S(1)}, u32[]{:S(2)}, u32[]{:S(2)}) collective-permute-start(f32[8,1,64]{2,1,0:T(1,128)S(1)} %get-tuple-element.124), channel_id=1, source_target_pairs={{0,1},{1,2},{2,3},{3,128},{128,129},{129,130},{130,131},{131,256},... | collective-permute-start | bytes 6152 | tf_op jit(solution)/shard_map/ppermute | solution.py:24
  545.5 14.5 %collective-permute-start.39 = (f32[8,1,64]{2,1,0:T(1,128)S(1)}, f32[8,1,64]{2,1,0:T(1,128)S(1)}, u32[]{:S(2)}, u32[]{:S(2)}) collective-permute-start(f32[8,1,64]{2,1,0:T(1,128)S(1)} %get-tuple-element.120), channel_id=1, source_target_pairs={{0,1},{1,2},{2,3},{3,128},{128,129},{129,130},{130,131},{131,256},... | collective-permute-start | bytes 6152 | tf_op jit(solution)/shard_map/ppermute | solution.py:24
  572.2 14.5 %collective-permute-start.43 = (f32[16,1,128]{2,1,0:T(1,128)S(1)}, f32[16,1,128]{2,1,0:T(1,128)S(1)}, u32[]{:S(2)}, u32[]{:S(2)}) collective-permute-start(f32[16,1,128]{2,1,0:T(1,128)S(1)} %get-tuple-element.88), channel_id=1, source_target_pairs={{0,1},{1,2},{2,3},{3,128},{128,129},{129,130},{130,131},{131,256},... | collective-permute-start | bytes 24584 | tf_op jit(solution)/shard_map/ppermute | solution.py:24
  598.6 14.5 %collective-permute-start.47 = (f32[16,1,128]{2,1,0:T(1,128)S(1)}, f32[16,1,128]{2,1,0:T(1,128)S(1)}, u32[]{:S(2)}, u32[]{:S(2)}) collective-permute-start(f32[16,1,128]{2,1,0:T(1,128)S(1)} %get-tuple-element.84), channel_id=1, source_target_pairs={{0,1},{1,2},{2,3},{3,128},{128,129},{129,130},{130,131},{131,256},... | collective-permute-start | bytes 24584 | tf_op jit(solution)/shard_map/ppermute | solution.py:24
  624.9 14.5 %collective-permute-start.51 = (f32[16,1,128]{2,1,0:T(1,128)S(1)}, f32[16,1,128]{2,1,0:T(1,128)S(1)}, u32[]{:S(2)}, u32[]{:S(2)}) collective-permute-start(f32[16,1,128]{2,1,0:T(1,128)S(1)} %get-tuple-element.80), channel_id=1, source_target_pairs={{0,1},{1,2},{2,3},{3,128},{128,129},{129,130},{130,131},{131,256},... | collective-permute-start | bytes 24584 | tf_op jit(solution)/shard_map/ppermute | solution.py:24
  651.3 14.5 %collective-permute-start.55 = (f32[16,1,128]{2,1,0:T(1,128)S(1)}, f32[16,1,128]{2,1,0:T(1,128)S(1)}, u32[]{:S(2)}, u32[]{:S(2)}) collective-permute-start(f32[16,1,128]{2,1,0:T(1,128)S(1)} %get-tuple-element.76), channel_id=1, source_target_pairs={{0,1},{1,2},{2,3},{3,128},{128,129},{129,130},{130,131},{131,256},... | collective-permute-start | bytes 24584 | tf_op jit(solution)/shard_map/ppermute | solution.py:24
  731.1 14.5 %collective-permute-start.63 = (f32[8,1,64]{2,1,0:T(1,128)S(1)}, f32[8,1,64]{2,1,0:T(1,128)S(1)}, u32[]{:S(2)}, u32[]{:S(2)}) collective-permute-start(f32[8,1,64]{2,1,0:T(1,128)S(1)} %get-tuple-element.116), channel_id=1, source_target_pairs={{0,1},{1,2},{2,3},{3,128},{128,129},{129,130},{130,131},{131,256},... | collective-permute-start | bytes 6152 | tf_op jit(solution)/shard_map/ppermute | solution.py:24
  763.7 14.5 %collective-permute-start.67 = (f32[8,1,64]{2,1,0:T(1,128)S(1)}, f32[8,1,64]{2,1,0:T(1,128)S(1)}, u32[]{:S(2)}, u32[]{:S(2)}) collective-permute-start(f32[8,1,64]{2,1,0:T(1,128)S(1)} %get-tuple-element.112), channel_id=1, source_target_pairs={{0,1},{1,2},{2,3},{3,128},{128,129},{129,130},{130,131},{131,256},... | collective-permute-start | bytes 6152 | tf_op jit(solution)/shard_map/ppermute | solution.py:24
  792.7 14.5 %collective-permute-start.71 = (f32[4,1,32]{2,0,1:T(4,128)S(1)}, f32[4,1,32]{2,0,1:T(4,128)S(1)}, u32[]{:S(2)}, u32[]{:S(2)}) collective-permute-start(f32[4,1,32]{2,0,1:T(4,128)S(1)} %get-tuple-element.144), channel_id=1, source_target_pairs={{0,1},{1,2},{2,3},{3,128},{128,129},{129,130},{130,131},{131,256},... | collective-permute-start | bytes 1544 | tf_op jit(solution)/shard_map/ppermute | solution.py:24
  818.9 14.5 %collective-permute-start.75 = (f32[4,1,32]{2,0,1:T(4,128)S(1)}, f32[4,1,32]{2,0,1:T(4,128)S(1)}, u32[]{:S(2)}, u32[]{:S(2)}) collective-permute-start(f32[4,1,32]{2,0,1:T(4,128)S(1)} %get-tuple-element.140), channel_id=1, source_target_pairs={{0,1},{1,2},{2,3},{3,128},{128,129},{129,130},{130,131},{131,256},... | collective-permute-start | bytes 1544 | tf_op jit(solution)/shard_map/ppermute | solution.py:24
  884.9 14.5 %collective-permute-start.79 = (f32[4,1,32]{2,0,1:T(4,128)S(1)}, f32[4,1,32]{2,0,1:T(4,128)S(1)}, u32[]{:S(2)}, u32[]{:S(2)}) collective-permute-start(f32[4,1,32]{2,0,1:T(4,128)S(1)} %get-tuple-element.136), channel_id=1, source_target_pairs={{0,1},{1,2},{2,3},{3,128},{128,129},{129,130},{130,131},{131,256},... | collective-permute-start | bytes 1544 | tf_op jit(solution)/shard_map/ppermute | solution.py:24
  939.9 14.5 %collective-permute-start.87 = (f32[8,1,64]{2,1,0:T(1,128)S(1)}, f32[8,1,64]{2,1,0:T(1,128)S(1)}, u32[]{:S(2)}, u32[]{:S(2)}) collective-permute-start(f32[8,1,64]{2,1,0:T(1,128)S(1)} %get-tuple-element.104), channel_id=1, source_target_pairs={{0,1},{1,2},{2,3},{3,128},{128,129},{129,130},{130,131},{131,256},... | collective-permute-start | bytes 6152 | tf_op jit(solution)/shard_map/ppermute | solution.py:24
  1027.0 17.8 %fusion.8 = f32[16,32,512]{2,1,0:T(8,128)} fusion(f32[16,32,512]{1,2,0:T(8,128)S(1)} %bitcast.160), kind=kOutput, calls=%fused_computation.19 | convolution fusion | flops 1614544896 | bytes 2097152 | tf_op jit(solution)/shard_map/abj,kj->abk/dot_general | solution.py:58
  (473 shorter events, 627.3 us)
Async XLA Ops:
  13.9 28.6 %all-to-all-start.2 = ((f32[32,1,512]{2,1,0:T(1,128)}), f32[32,1,512]{2,1,0:T(1,128)S(1)}, u32[]{:S(2)}, u32[]{:S(2)}) async-start(f32[32,1,512]{2,1,0:T(1,128)} %reshape.359), calls=%async_computation.2 | async-start | bytes 131072 | tf_op jit(solution)/shard_map/all_to_all | solution.py:139
  42.5 58.7 %all-to-all-start = ((f32[32,1,8192]{2,1,0:T(1,128)}), f32[32,1,8192]{2,1,0:T(1,128)S(1)}, u32[]{:S(2)}, u32[]{:S(2)}) async-start(f32[32,1,8192]{2,1,0:T(1,128)} %reshape.355), calls=%async_computation | async-start | bytes 2097152 | tf_op jit(solution)/shard_map/all_to_all | solution.py:138
  101.2 47.3 %all-to-all-start.3 = ((f32[16,1,2048]{2,1,0:T(1,128)}), f32[16,1,2048]{2,1,0:T(1,128)S(1)}, u32[]{:S(2)}, u32[]{:S(2)}) async-start(f32[16,1,2048]{2,1,0:T(1,128)} %reshape.361), calls=%async_computation.3 | async-start | bytes 262144 | tf_op jit(solution)/shard_map/all_to_all | solution.py:145
  148.6 69.1 %all-to-all-start.1 = ((f32[16,1,16384]{2,1,0:T(1,128)}), f32[16,1,16384]{2,1,0:T(1,128)S(1)}, u32[]{:S(2)}, u32[]{:S(2)}) async-start(f32[16,1,16384]{2,1,0:T(1,128)} %reshape.357), calls=%async_computation.1 | async-start | bytes 2097152 | tf_op jit(solution)/shard_map/all_to_all | solution.py:144
  291.6 25.2 %collective-permute-start.1 = (f32[1,8,128]{2,1,0:T(8,128)S(1)}, f32[1,8,128]{2,1,0:T(8,128)S(1)}, u32[]{:S(2)}, u32[]{:S(2)}) collective-permute-start(f32[1,8,128]{2,1,0:T(8,128)S(1)} %copy.619), channel_id=1, source_target_pairs={{0,4},{4,8},{8,12},{12,16},{16,20},{20,24},{24,28},{28,32},{32,36}... | collective-permute-start | bytes 12296 | tf_op jit(solution)/shard_map/ppermute | solution.py:24
  293.8 23.7 %collective-permute-start.3 = (f32[16,1,128]{2,1,0:T(1,128)S(1)}, f32[16,1,128]{2,1,0:T(1,128)S(1)}, u32[]{:S(2)}, u32[]{:S(2)}) collective-permute-start(f32[16,1,128]{2,1,0:T(1,128)S(1)} %get-tuple-element.99), channel_id=1, source_target_pairs={{1,0},{2,1},{3,2},{128,3},{129,128},{130,129},{131,130},{256,131},... | collective-permute-start | bytes 24584 | tf_op jit(solution)/shard_map/ppermute | solution.py:25
  319.6 25.3 %collective-permute-start.6 = (f32[16,1,128]{2,1,0:T(1,128)S(1)}, f32[16,1,128]{2,1,0:T(1,128)S(1)}, u32[]{:S(2)}, u32[]{:S(2)}) collective-permute-start(f32[16,1,128]{2,1,0:T(1,128)S(1)} %get-tuple-element.97), channel_id=1, source_target_pairs={{1,0},{2,1},{3,2},{128,3},{129,128},{130,129},{131,130},{256,131},... | collective-permute-start | bytes 24584 | tf_op jit(solution)/shard_map/ppermute | solution.py:25
  321.5 23.4 %collective-permute-start.7 = (f32[16,1,128]{2,1,0:T(1,128)S(1)}, f32[16,1,128]{2,1,0:T(1,128)S(1)}, u32[]{:S(2)}, u32[]{:S(2)}) collective-permute-start(f32[16,1,128]{2,1,0:T(1,128)S(1)} %get-tuple-element.96), channel_id=1, source_target_pairs={{0,1},{1,2},{2,3},{3,128},{128,129},{129,130},{130,131},{131,256},... | collective-permute-start | bytes 24584 | tf_op jit(solution)/shard_map/ppermute | solution.py:24
  351.0 21.9 %collective-permute-start.10 = (f32[16,1,128]{2,1,0:T(1,128)S(1)}, f32[16,1,128]{2,1,0:T(1,128)S(1)}, u32[]{:S(2)}, u32[]{:S(2)}) collective-permute-start(f32[16,1,128]{2,1,0:T(1,128)S(1)} %get-tuple-element.93), channel_id=1, source_target_pairs={{1,0},{2,1},{3,2},{128,3},{129,128},{130,129},{131,130},{256,131},... | collective-permute-start | bytes 24584 | tf_op jit(solution)/shard_map/ppermute | solution.py:25
  385.6 21.7 %collective-permute-start.14 = (f32[8,1,64]{2,1,0:T(1,128)S(1)}, f32[8,1,64]{2,1,0:T(1,128)S(1)}, u32[]{:S(2)}, u32[]{:S(2)}) collective-permute-start(f32[8,1,64]{2,1,0:T(1,128)S(1)} %get-tuple-element.133), channel_id=1, source_target_pairs={{1,0},{2,1},{3,2},{128,3},{129,128},{130,129},{131,130},{256,131},... | collective-permute-start | bytes 6152 | tf_op jit(solution)/shard_map/ppermute | solution.py:25
  438.7 21.7 %collective-permute-start.22 = (f32[4,1,32]{2,0,1:T(4,128)S(1)}, f32[4,1,32]{2,0,1:T(4,128)S(1)}, u32[]{:S(2)}, u32[]{:S(2)}) collective-permute-start(f32[4,1,32]{2,0,1:T(4,128)S(1)} %get-tuple-element.157), channel_id=1, source_target_pairs={{1,0},{2,1},{3,2},{128,3},{129,128},{130,129},{131,130},{256,131},... | collective-permute-start | bytes 1544 | tf_op jit(solution)/shard_map/ppermute | solution.py:25
  517.4 21.7 %collective-permute-start.34 = (f32[8,1,64]{2,1,0:T(1,128)S(1)}, f32[8,1,64]{2,1,0:T(1,128)S(1)}, u32[]{:S(2)}, u32[]{:S(2)}) collective-permute-start(f32[8,1,64]{2,1,0:T(1,128)S(1)} %get-tuple-element.125), channel_id=1, source_target_pairs={{1,0},{2,1},{3,2},{128,3},{129,128},{130,129},{131,130},{256,131},... | collective-permute-start | bytes 6152 | tf_op jit(solution)/shard_map/ppermute | solution.py:25
  649.4 41.3 %collective-permute-start.54 = (f32[16,1,128]{2,1,0:T(1,128)S(1)}, f32[16,1,128]{2,1,0:T(1,128)S(1)}, u32[]{:S(2)}, u32[]{:S(2)}) collective-permute-start(f32[16,1,128]{2,1,0:T(1,128)S(1)} %get-tuple-element.77), channel_id=1, source_target_pairs={{1,0},{2,1},{3,2},{128,3},{129,128},{130,129},{131,130},{256,131},... | collective-permute-start | bytes 24584 | tf_op jit(solution)/shard_map/ppermute | solution.py:25
  651.3 39.4 %collective-permute-start.55 = (f32[16,1,128]{2,1,0:T(1,128)S(1)}, f32[16,1,128]{2,1,0:T(1,128)S(1)}, u32[]{:S(2)}, u32[]{:S(2)}) collective-permute-start(f32[16,1,128]{2,1,0:T(1,128)S(1)} %get-tuple-element.76), channel_id=1, source_target_pairs={{0,1},{1,2},{2,3},{3,128},{128,129},{129,130},{130,131},{131,256},... | collective-permute-start | bytes 24584 | tf_op jit(solution)/shard_map/ppermute | solution.py:24
  665.8 24.9 %collective-permute-start.52 = (f32[1,8,128]{2,1,0:T(8,128)S(1)}, f32[1,8,128]{2,1,0:T(8,128)S(1)}, u32[]{:S(2)}, u32[]{:S(2)}) collective-permute-start(f32[1,8,128]{2,1,0:T(8,128)S(1)} %get-tuple-element.75), channel_id=1, source_target_pairs={{4,0},{8,4},{12,8},{16,12},{20,16},{24,20},{28,24},{32,28},{36,32}... | collective-permute-start | bytes 12296 | tf_op jit(solution)/shard_map/ppermute | solution.py:25
  667.7 23.0 %collective-permute-start.53 = (f32[1,8,128]{2,1,0:T(8,128)S(1)}, f32[1,8,128]{2,1,0:T(8,128)S(1)}, u32[]{:S(2)}, u32[]{:S(2)}) collective-permute-start(f32[1,8,128]{2,1,0:T(8,128)S(1)} %get-tuple-element.74), channel_id=1, source_target_pairs={{0,4},{4,8},{8,12},{12,16},{16,20},{20,24},{24,28},{28,32},{32,36}... | collective-permute-start | bytes 12296 | tf_op jit(solution)/shard_map/ppermute | solution.py:24
  686.4 156.6 %all-to-all-start.4 = ((f32[16,1,16384]{2,1,0:T(1,128)}), f32[16,1,16384]{2,1,0:T(1,128)S(1)}, u32[]{:S(2)}, u32[]{:S(2)}) async-start(f32[16,1,16384]{2,1,0:T(1,128)} %reshape.363), calls=%async_computation.4 | async-start | bytes 2097152 | tf_op jit(solution)/shard_map/all_to_all | solution.py:158
  691.1 23.6 %collective-permute-start.58 = (f32[16,1,128]{2,1,0:T(1,128)S(1)}, f32[16,1,128]{2,1,0:T(1,128)S(1)}, u32[]{:S(2)}, u32[]{:S(2)}) collective-permute-start(f32[16,1,128]{2,1,0:T(1,128)S(1)} %get-tuple-element.73), channel_id=1, source_target_pairs={{1,0},{2,1},{3,2},{128,3},{129,128},{130,129},{131,130},{256,131},... | collective-permute-start | bytes 24584 | tf_op jit(solution)/shard_map/ppermute | solution.py:25
  729.2 21.7 %collective-permute-start.62 = (f32[8,1,64]{2,1,0:T(1,128)S(1)}, f32[8,1,64]{2,1,0:T(1,128)S(1)}, u32[]{:S(2)}, u32[]{:S(2)}) collective-permute-start(f32[8,1,64]{2,1,0:T(1,128)S(1)} %get-tuple-element.117), channel_id=1, source_target_pairs={{1,0},{2,1},{3,2},{128,3},{129,128},{130,129},{131,130},{256,131},... | collective-permute-start | bytes 6152 | tf_op jit(solution)/shard_map/ppermute | solution.py:25
  761.8 22.4 %collective-permute-start.66 = (f32[8,1,64]{2,1,0:T(1,128)S(1)}, f32[8,1,64]{2,1,0:T(1,128)S(1)}, u32[]{:S(2)}, u32[]{:S(2)}) collective-permute-start(f32[8,1,64]{2,1,0:T(1,128)S(1)} %get-tuple-element.113), channel_id=1, source_target_pairs={{1,0},{2,1},{3,2},{128,3},{129,128},{130,129},{131,130},{256,131},... | collective-permute-start | bytes 6152 | tf_op jit(solution)/shard_map/ppermute | solution.py:25
  790.8 21.7 %collective-permute-start.70 = (f32[4,1,32]{2,0,1:T(4,128)S(1)}, f32[4,1,32]{2,0,1:T(4,128)S(1)}, u32[]{:S(2)}, u32[]{:S(2)}) collective-permute-start(f32[4,1,32]{2,0,1:T(4,128)S(1)} %get-tuple-element.145), channel_id=1, source_target_pairs={{1,0},{2,1},{3,2},{128,3},{129,128},{130,129},{131,130},{256,131},... | collective-permute-start | bytes 1544 | tf_op jit(solution)/shard_map/ppermute | solution.py:25
  874.5 143.6 %all-to-all-start.5 = ((f32[32,1,8192]{2,1,0:T(1,128)}), f32[32,1,8192]{2,1,0:T(1,128)S(1)}, u32[]{:S(2)}, u32[]{:S(2)}) async-start(f32[32,1,8192]{2,1,0:T(1,128)} %reshape.365), calls=%async_computation.5 | async-start | bytes 2097152 | tf_op jit(solution)/shard_map/all_to_all | solution.py:164
  883.0 22.6 %collective-permute-start.78 = (f32[4,1,32]{2,0,1:T(4,128)S(1)}, f32[4,1,32]{2,0,1:T(4,128)S(1)}, u32[]{:S(2)}, u32[]{:S(2)}) collective-permute-start(f32[4,1,32]{2,0,1:T(4,128)S(1)} %get-tuple-element.137), channel_id=1, source_target_pairs={{1,0},{2,1},{3,2},{128,3},{129,128},{130,129},{131,130},{256,131},... | collective-permute-start | bytes 1544 | tf_op jit(solution)/shard_map/ppermute | solution.py:25
  938.0 21.7 %collective-permute-start.86 = (f32[8,1,64]{2,1,0:T(1,128)S(1)}, f32[8,1,64]{2,1,0:T(1,128)S(1)}, u32[]{:S(2)}, u32[]{:S(2)}) collective-permute-start(f32[8,1,64]{2,1,0:T(1,128)S(1)} %get-tuple-element.105), channel_id=1, source_target_pairs={{1,0},{2,1},{3,2},{128,3},{129,128},{130,129},{131,130},{256,131},... | collective-permute-start | bytes 6152 | tf_op jit(solution)/shard_map/ppermute | solution.py:25
  (84 other events, 1121.3 us)
where the time goes:
time: 1060 us; the launch traced here: 1050 us
  starting transfers between devices  608 us (57%)
  waiting for transfers between devices  200 us (19%)
  local copies, waits for them, and re-layouts  120 us (11%)
  matrix products  61.1 us (6%)
  other arithmetic  32.9 us (3%)
  blocking collectives  18.9 us (2%)
    ppermute x48, starting transfers between devices, extended(): lax.ppermute(last, axis, up)  420 us
    ppermute x48, starting transfers between devices, extended(): lax.ppermute(initial, axis, [(b, a) for a, b in up])  111 us
    ppermute x48, waiting for transfers between devices, extended(): lax.ppermute(last, axis, up)  105 us
    all_to_all x1, waiting for transfers between devices, local(): lax.all_to_all(dense, ('group', 'gy'), split_axis=0, concat_axis=1, tiled...  50.5 us
    unnamed x26, local copies, waits for them, and re-layouts  37.8 us
    all_to_all x1, waiting for transfers between devices, local(): lax.all_to_all(dense, 'gx', split_axis=2, concat_axis=0, tiled=True)  37.1 us
    dot_general x4, matrix products, last_axis(): return jnp.einsum('abj,kj->abk', block, table, precision=HIGH)  26.1 us
  transfers between devices with their start and end apart: 103, of which 27 were waited for; matrix products, arithmetic and copies ran while one was open for 9% of the time, Pallas kernels for 0%

commit v1 on v0

--- a/solution.py
+++ b/solution.py
@@ -134,8 +134,20 @@
     z_table = cas_table(wave, offsets[2] + jnp.arange(rest.shape[2], dtype=jnp.int32), NP)
     dense = last_axis(parent_mass, full)
     light = last_axis(rest, z_table)
+
+    def domain_choose(payload):
+        return jnp.concatenate(
+            lax.all_to_all(
+                jnp.stack(jnp.split(payload, lax.axis_size("gx"), 2)),
+                axis_name="gx",
+                split_axis=0,
+                concat_axis=0,
+            ),
+            0,
+        )
+
     dense, light = (
-        lax.all_to_all(dense, "gx", split_axis=2, concat_axis=0, tiled=True),
+        domain_choose(dense),
         lax.all_to_all(light, "gx", split_axis=2, concat_axis=0, tiled=True),
     )
     dense = first_axis(dense, full)

time: 1060 us -> 1090 us (1.028)
  local copies, waits for them, and re-layouts: 120 us -> 151 us
  starting transfers between devices: 608 us -> 597 us
    unnamed x26 -> x55, local copies, waits for them, and re-layouts: 37.8 us -> 63.6 us
    another operation x2 -> x5, local copies, waits for them, and re-layouts: 0.59 us -> 16 us  [the longest x1 7.77 us: first_axis(): product = jnp.dot(table, block.reshape(block.shape[0], -1), precision=HIGH)]
  transfers between devices with their start and end apart: 103 -> 103, of which waited for: 27 -> 29; matrix products, arithmetic and copies ran while one was open for 9% -> 11% of each run, Pallas kernels for 0% -> 0%
where the time goes in v1:
time: 1090 us; the launch traced here: 1070 us
  starting transfers between devices  597 us (55%)
  waiting for transfers between devices  209 us (19%)
  local copies, waits for them, and re-layouts  151 us (14%)
  matrix products  61.1 us (6%)
  other arithmetic  32.9 us (3%)
  blocking collectives  18.9 us (2%)
    ppermute x48, starting transfers between devices, extended(): lax.ppermute(last, axis, up)  413 us
    ppermute x48, starting transfers between devices, extended(): lax.ppermute(initial, axis, [(b, a) for a, b in up])  110 us
    ppermute x48, waiting for transfers between devices, extended(): lax.ppermute(last, axis, up)  106 us
    unnamed x55, local copies, waits for them, and re-layouts  63.6 us
    all_to_all x1, waiting for transfers between devices, local(): lax.all_to_all(dense, ('group', 'gy'), split_axis=0, concat_axis=1, tiled...  50.6 us
    all_to_all x1, waiting for transfers between devices, domain_choose(): lax.all_to_all(jnp.stack(jnp.split(payload, lax.axis_size('gx'), 2)), axi...  37.3 us
    dot_general x4, matrix products, last_axis(): return jnp.einsum('abj,kj->abk', block, table, precision=HIGH)  26.1 us
  transfers between devices with their start and end apart: 103, of which 29 were waited for; matrix products, arithmetic and copies ran while one was open for 11% of the time, Pallas kernels for 0%

profile of v1, /device:TPU:135, one launch (start us, length us, event | category | flops | bytes accessed | tf_op | source)
XLA Modules:
  0.0 1073.1 jit_solution(9331620526960282947)
XLA Ops:
  93.9 37.3 %all-to-all-done = f32[32,1,8192]{2,1,0:T(1,128)S(1)} async-done(((f32[32,1,8192]{2,1,0:T(1,128)}), f32[32,1,8192]{2,1,0:T(1,128)S(1)}, u32[]{:S(2)}, u32[]{:S(2)}) %all-to-all-start) | async-done | bytes 1048608 | tf_op jit(solution)/shard_map/all_to_all | solution.py:140
  178.5 14.7 %all-to-all-start.1 = ((f32[16,1,16384]{2,1,0:T(1,128)}), f32[16,1,16384]{2,1,0:T(1,128)S(1)}, u32[]{:S(2)}, u32[]{:S(2)}) async-start(f32[16,1,16384]{2,1,0:T(1,128)} %reshape.352), calls=%async_computation.1 | async-start | bytes 2097152 | tf_op jit(solution)/shard_map/all_to_all | solution.py:156
  197.0 50.6 %all-to-all-done.1 = f32[16,1,16384]{2,1,0:T(1,128)S(1)} async-done(((f32[16,1,16384]{2,1,0:T(1,128)}), f32[16,1,16384]{2,1,0:T(1,128)S(1)}, u32[]{:S(2)}, u32[]{:S(2)}) %all-to-all-start.1) | async-done | bytes 1048608 | tf_op jit(solution)/shard_map/all_to_all | solution.py:156
  274.9 18.9 %all_to_all.122 = f32[16,1,2048]{2,1,0:T(1,128)S(1)} all-to-all(f32[16,1,2048]{2,1,0:T(1,128)S(1)} %reshape.362), channel_id=1, replica_groups=mesh['group'=4,'gx'=32,'gy'=4] {'group','gy'}, dimensions={0} | all-to-all | bytes 262144 | tf_op jit(solution)/shard_map/all_to_all | solution.py:171
  350.3 14.5 %collective-permute-start.7 = (f32[16,1,128]{2,1,0:T(1,128)S(1)}, f32[16,1,128]{2,1,0:T(1,128)S(1)}, u32[]{:S(2)}, u32[]{:S(2)}) collective-permute-start(f32[16,1,128]{2,1,0:T(1,128)S(1)} %get-tuple-element.96), channel_id=1, source_target_pairs={{0,1},{1,2},{2,3},{3,128},{128,129},{129,130},{130,131},{131,256},... | collective-permute-start | bytes 24584 | tf_op jit(solution)/shard_map/ppermute | solution.py:24
  381.2 14.5 %collective-permute-start.11 = (f32[16,1,128]{2,1,0:T(1,128)S(1)}, f32[16,1,128]{2,1,0:T(1,128)S(1)}, u32[]{:S(2)}, u32[]{:S(2)}) collective-permute-start(f32[16,1,128]{2,1,0:T(1,128)S(1)} %get-tuple-element.92), channel_id=1, source_target_pairs={{0,1},{1,2},{2,3},{3,128},{128,129},{129,130},{130,131},{131,256},... | collective-permute-start | bytes 24584 | tf_op jit(solution)/shard_map/ppermute | solution.py:24
  415.8 14.5 %collective-permute-start.15 = (f32[8,1,64]{2,1,0:T(1,128)S(1)}, f32[8,1,64]{2,1,0:T(1,128)S(1)}, u32[]{:S(2)}, u32[]{:S(2)}) collective-permute-start(f32[8,1,64]{2,1,0:T(1,128)S(1)} %get-tuple-element.132), channel_id=1, source_target_pairs={{0,1},{1,2},{2,3},{3,128},{128,129},{129,130},{130,131},{131,256},... | collective-permute-start | bytes 6152 | tf_op jit(solution)/shard_map/ppermute | solution.py:24
  442.0 14.5 %collective-permute-start.19 = (f32[8,1,64]{2,1,0:T(1,128)S(1)}, f32[8,1,64]{2,1,0:T(1,128)S(1)}, u32[]{:S(2)}, u32[]{:S(2)}) collective-permute-start(f32[8,1,64]{2,1,0:T(1,128)S(1)} %get-tuple-element.128), channel_id=1, source_target_pairs={{0,1},{1,2},{2,3},{3,128},{128,129},{129,130},{130,131},{131,256},... | collective-permute-start | bytes 6152 | tf_op jit(solution)/shard_map/ppermute | solution.py:24
  468.9 14.5 %collective-permute-start.23 = (f32[4,1,32]{2,0,1:T(4,128)S(1)}, f32[4,1,32]{2,0,1:T(4,128)S(1)}, u32[]{:S(2)}, u32[]{:S(2)}) collective-permute-start(f32[4,1,32]{2,0,1:T(4,128)S(1)} %get-tuple-element.156), channel_id=1, source_target_pairs={{0,1},{1,2},{2,3},{3,128},{128,129},{129,130},{130,131},{131,256},... | collective-permute-start | bytes 1544 | tf_op jit(solution)/shard_map/ppermute | solution.py:24
  495.1 14.5 %collective-permute-start.27 = (f32[4,1,32]{2,0,1:T(4,128)S(1)}, f32[4,1,32]{2,0,1:T(4,128)S(1)}, u32[]{:S(2)}, u32[]{:S(2)}) collective-permute-start(f32[4,1,32]{2,0,1:T(4,128)S(1)} %get-tuple-element.152), channel_id=1, source_target_pairs={{0,1},{1,2},{2,3},{3,128},{128,129},{129,130},{130,131},{131,256},... | collective-permute-start | bytes 1544 | tf_op jit(solution)/shard_map/ppermute | solution.py:24
  521.2 14.5 %collective-permute-start.31 = (f32[4,1,32]{2,0,1:T(4,128)S(1)}, f32[4,1,32]{2,0,1:T(4,128)S(1)}, u32[]{:S(2)}, u32[]{:S(2)}) collective-permute-start(f32[4,1,32]{2,0,1:T(4,128)S(1)} %get-tuple-element.148), channel_id=1, source_target_pairs={{0,1},{1,2},{2,3},{3,128},{128,129},{129,130},{130,131},{131,256},... | collective-permute-start | bytes 1544 | tf_op jit(solution)/shard_map/ppermute | solution.py:24
  547.6 14.5 %collective-permute-start.35 = (f32[8,1,64]{2,1,0:T(1,128)S(1)}, f32[8,1,64]{2,1,0:T(1,128)S(1)}, u32[]{:S(2)}, u32[]{:S(2)}) collective-permute-start(f32[8,1,64]{2,1,0:T(1,128)S(1)} %get-tuple-element.124), channel_id=1, source_target_pairs={{0,1},{1,2},{2,3},{3,128},{128,129},{129,130},{130,131},{131,256},... | collective-permute-start | bytes 6152 | tf_op jit(solution)/shard_map/ppermute | solution.py:24
  573.8 14.5 %collective-permute-start.39 = (f32[8,1,64]{2,1,0:T(1,128)S(1)}, f32[8,1,64]{2,1,0:T(1,128)S(1)}, u32[]{:S(2)}, u32[]{:S(2)}) collective-permute-start(f32[8,1,64]{2,1,0:T(1,128)S(1)} %get-tuple-element.120), channel_id=1, source_target_pairs={{0,1},{1,2},{2,3},{3,128},{128,129},{129,130},{130,131},{131,256},... | collective-permute-start | bytes 6152 | tf_op jit(solution)/shard_map/ppermute | solution.py:24
  600.5 14.5 %collective-permute-start.43 = (f32[16,1,128]{2,1,0:T(1,128)S(1)}, f32[16,1,128]{2,1,0:T(1,128)S(1)}, u32[]{:S(2)}, u32[]{:S(2)}) collective-permute-start(f32[16,1,128]{2,1,0:T(1,128)S(1)} %get-tuple-element.88), channel_id=1, source_target_pairs={{0,1},{1,2},{2,3},{3,128},{128,129},{129,130},{130,131},{131,256},... | collective-permute-start | bytes 24584 | tf_op jit(solution)/shard_map/ppermute | solution.py:24
  626.9 14.5 %collective-permute-start.47 = (f32[16,1,128]{2,1,0:T(1,128)S(1)}, f32[16,1,128]{2,1,0:T(1,128)S(1)}, u32[]{:S(2)}, u32[]{:S(2)}) collective-permute-start(f32[16,1,128]{2,1,0:T(1,128)S(1)} %get-tuple-element.84), channel_id=1, source_target_pairs={{0,1},{1,2},{2,3},{3,128},{128,129},{129,130},{130,131},{131,256},... | collective-permute-start | bytes 24584 | tf_op jit(solution)/shard_map/ppermute | solution.py:24
  653.3 14.5 %collective-permute-start.51 = (f32[16,1,128]{2,1,0:T(1,128)S(1)}, f32[16,1,128]{2,1,0:T(1,128)S(1)}, u32[]{:S(2)}, u32[]{:S(2)}) collective-permute-start(f32[16,1,128]{2,1,0:T(1,128)S(1)} %get-tuple-element.80), channel_id=1, source_target_pairs={{0,1},{1,2},{2,3},{3,128},{128,129},{129,130},{130,131},{131,256},... | collective-permute-start | bytes 24584 | tf_op jit(solution)/shard_map/ppermute | solution.py:24
  679.6 14.5 %collective-permute-start.55 = (f32[16,1,128]{2,1,0:T(1,128)S(1)}, f32[16,1,128]{2,1,0:T(1,128)S(1)}, u32[]{:S(2)}, u32[]{:S(2)}) collective-permute-start(f32[16,1,128]{2,1,0:T(1,128)S(1)} %get-tuple-element.76), channel_id=1, source_target_pairs={{0,1},{1,2},{2,3},{3,128},{128,129},{129,130},{130,131},{131,256},... | collective-permute-start | bytes 24584 | tf_op jit(solution)/shard_map/ppermute | solution.py:24
  759.5 14.5 %collective-permute-start.63 = (f32[8,1,64]{2,1,0:T(1,128)S(1)}, f32[8,1,64]{2,1,0:T(1,128)S(1)}, u32[]{:S(2)}, u32[]{:S(2)}) collective-permute-start(f32[8,1,64]{2,1,0:T(1,128)S(1)} %get-tuple-element.116), channel_id=1, source_target_pairs={{0,1},{1,2},{2,3},{3,128},{128,129},{129,130},{130,131},{131,256},... | collective-permute-start | bytes 6152 | tf_op jit(solution)/shard_map/ppermute | solution.py:24
  793.2 14.5 %collective-permute-start.67 = (f32[8,1,64]{2,1,0:T(1,128)S(1)}, f32[8,1,64]{2,1,0:T(1,128)S(1)}, u32[]{:S(2)}, u32[]{:S(2)}) collective-permute-start(f32[8,1,64]{2,1,0:T(1,128)S(1)} %get-tuple-element.112), channel_id=1, source_target_pairs={{0,1},{1,2},{2,3},{3,128},{128,129},{129,130},{130,131},{131,256},... | collective-permute-start | bytes 6152 | tf_op jit(solution)/shard_map/ppermute | solution.py:24
  822.1 14.5 %collective-permute-start.71 = (f32[4,1,32]{2,0,1:T(4,128)S(1)}, f32[4,1,32]{2,0,1:T(4,128)S(1)}, u32[]{:S(2)}, u32[]{:S(2)}) collective-permute-start(f32[4,1,32]{2,0,1:T(4,128)S(1)} %get-tuple-element.144), channel_id=1, source_target_pairs={{0,1},{1,2},{2,3},{3,128},{128,129},{129,130},{130,131},{131,256},... | collective-permute-start | bytes 1544 | tf_op jit(solution)/shard_map/ppermute | solution.py:24
  848.3 14.5 %collective-permute-start.75 = (f32[4,1,32]{2,0,1:T(4,128)S(1)}, f32[4,1,32]{2,0,1:T(4,128)S(1)}, u32[]{:S(2)}, u32[]{:S(2)}) collective-permute-start(f32[4,1,32]{2,0,1:T(4,128)S(1)} %get-tuple-element.140), channel_id=1, source_target_pairs={{0,1},{1,2},{2,3},{3,128},{128,129},{129,130},{130,131},{131,256},... | collective-permute-start | bytes 1544 | tf_op jit(solution)/shard_map/ppermute | solution.py:24
  913.0 14.5 %collective-permute-start.79 = (f32[4,1,32]{2,0,1:T(4,128)S(1)}, f32[4,1,32]{2,0,1:T(4,128)S(1)}, u32[]{:S(2)}, u32[]{:S(2)}) collective-permute-start(f32[4,1,32]{2,0,1:T(4,128)S(1)} %get-tuple-element.136), channel_id=1, source_target_pairs={{0,1},{1,2},{2,3},{3,128},{128,129},{129,130},{130,131},{131,256},... | collective-permute-start | bytes 1544 | tf_op jit(solution)/shard_map/ppermute | solution.py:24
  968.0 14.5 %collective-permute-start.87 = (f32[8,1,64]{2,1,0:T(1,128)S(1)}, f32[8,1,64]{2,1,0:T(1,128)S(1)}, u32[]{:S(2)}, u32[]{:S(2)}) collective-permute-start(f32[8,1,64]{2,1,0:T(1,128)S(1)} %get-tuple-element.104), channel_id=1, source_target_pairs={{0,1},{1,2},{2,3},{3,128},{128,129},{129,130},{130,131},{131,256},... | collective-permute-start | bytes 6152 | tf_op jit(solution)/shard_map/ppermute | solution.py:24
  1055.1 17.8 %fusion.8 = f32[16,32,512]{2,1,0:T(8,128)} fusion(f32[16,32,512]{1,2,0:T(8,128)S(1)} %bitcast.285), kind=kOutput, calls=%fused_computation.19 | convolution fusion | flops 1614544896 | bytes 2097152 | tf_op jit(solution)/shard_map/abj,kj->abk/dot_general | solution.py:58
  (503 shorter events, 655.1 us)
Async XLA Ops:
  14.6 58.4 %all-to-all-start.2 = ((f32[32,1,512]{2,1,0:T(1,128)}), f32[32,1,512]{2,1,0:T(1,128)S(1)}, u32[]{:S(2)}, u32[]{:S(2)}) async-start(f32[32,1,512]{2,1,0:T(1,128)} %reshape.354), calls=%async_computation.2 | async-start | bytes 131072 | tf_op jit(solution)/shard_map/all_to_all | solution.py:151
  72.9 58.3 %all-to-all-start = ((f32[32,1,8192]{2,1,0:T(1,128)}), f32[32,1,8192]{2,1,0:T(1,128)S(1)}, u32[]{:S(2)}, u32[]{:S(2)}) async-start(f32[32,1,8192]{2,1,0:T(1,128)} %reshape.350), calls=%async_computation | async-start | bytes 2097152 | tf_op jit(solution)/shard_map/all_to_all | solution.py:140
  131.2 47.3 %all-to-all-start.3 = ((f32[16,1,2048]{2,1,0:T(1,128)}), f32[16,1,2048]{2,1,0:T(1,128)S(1)}, u32[]{:S(2)}, u32[]{:S(2)}) async-start(f32[16,1,2048]{2,1,0:T(1,128)} %reshape.356), calls=%async_computation.3 | async-start | bytes 262144 | tf_op jit(solution)/shard_map/all_to_all | solution.py:157
  178.5 69.1 %all-to-all-start.1 = ((f32[16,1,16384]{2,1,0:T(1,128)}), f32[16,1,16384]{2,1,0:T(1,128)S(1)}, u32[]{:S(2)}, u32[]{:S(2)}) async-start(f32[16,1,16384]{2,1,0:T(1,128)} %reshape.352), calls=%async_computation.1 | async-start | bytes 2097152 | tf_op jit(solution)/shard_map/all_to_all | solution.py:156
  348.4 24.8 %collective-permute-start.6 = (f32[16,1,128]{2,1,0:T(1,128)S(1)}, f32[16,1,128]{2,1,0:T(1,128)S(1)}, u32[]{:S(2)}, u32[]{:S(2)}) collective-permute-start(f32[16,1,128]{2,1,0:T(1,128)S(1)} %get-tuple-element.97), channel_id=1, source_target_pairs={{1,0},{2,1},{3,2},{128,3},{129,128},{130,129},{131,130},{256,131},... | collective-permute-start | bytes 24584 | tf_op jit(solution)/shard_map/ppermute | solution.py:25
  350.3 22.9 %collective-permute-start.7 = (f32[16,1,128]{2,1,0:T(1,128)S(1)}, f32[16,1,128]{2,1,0:T(1,128)S(1)}, u32[]{:S(2)}, u32[]{:S(2)}) collective-permute-start(f32[16,1,128]{2,1,0:T(1,128)S(1)} %get-tuple-element.96), channel_id=1, source_target_pairs={{0,1},{1,2},{2,3},{3,128},{128,129},{129,130},{130,131},{131,256},... | collective-permute-start | bytes 24584 | tf_op jit(solution)/shard_map/ppermute | solution.py:24
  379.3 21.9 %collective-permute-start.10 = (f32[16,1,128]{2,1,0:T(1,128)S(1)}, f32[16,1,128]{2,1,0:T(1,128)S(1)}, u32[]{:S(2)}, u32[]{:S(2)}) collective-permute-start(f32[16,1,128]{2,1,0:T(1,128)S(1)} %get-tuple-element.93), channel_id=1, source_target_pairs={{1,0},{2,1},{3,2},{128,3},{129,128},{130,129},{131,130},{256,131},... | collective-permute-start | bytes 24584 | tf_op jit(solution)/shard_map/ppermute | solution.py:25
  413.9 21.7 %collective-permute-start.14 = (f32[8,1,64]{2,1,0:T(1,128)S(1)}, f32[8,1,64]{2,1,0:T(1,128)S(1)}, u32[]{:S(2)}, u32[]{:S(2)}) collective-permute-start(f32[8,1,64]{2,1,0:T(1,128)S(1)} %get-tuple-element.133), channel_id=1, source_target_pairs={{1,0},{2,1},{3,2},{128,3},{129,128},{130,129},{131,130},{256,131},... | collective-permute-start | bytes 6152 | tf_op jit(solution)/shard_map/ppermute | solution.py:25
  440.1 21.7 %collective-permute-start.18 = (f32[8,1,64]{2,1,0:T(1,128)S(1)}, f32[8,1,64]{2,1,0:T(1,128)S(1)}, u32[]{:S(2)}, u32[]{:S(2)}) collective-permute-start(f32[8,1,64]{2,1,0:T(1,128)S(1)} %get-tuple-element.129), channel_id=1, source_target_pairs={{1,0},{2,1},{3,2},{128,3},{129,128},{130,129},{131,130},{256,131},... | collective-permute-start | bytes 6152 | tf_op jit(solution)/shard_map/ppermute | solution.py:25
  467.0 21.7 %collective-permute-start.22 = (f32[4,1,32]{2,0,1:T(4,128)S(1)}, f32[4,1,32]{2,0,1:T(4,128)S(1)}, u32[]{:S(2)}, u32[]{:S(2)}) collective-permute-start(f32[4,1,32]{2,0,1:T(4,128)S(1)} %get-tuple-element.157), channel_id=1, source_target_pairs={{1,0},{2,1},{3,2},{128,3},{129,128},{130,129},{131,130},{256,131},... | collective-permute-start | bytes 1544 | tf_op jit(solution)/shard_map/ppermute | solution.py:25
  545.7 21.7 %collective-permute-start.34 = (f32[8,1,64]{2,1,0:T(1,128)S(1)}, f32[8,1,64]{2,1,0:T(1,128)S(1)}, u32[]{:S(2)}, u32[]{:S(2)}) collective-permute-start(f32[8,1,64]{2,1,0:T(1,128)S(1)} %get-tuple-element.125), channel_id=1, source_target_pairs={{1,0},{2,1},{3,2},{128,3},{129,128},{130,129},{131,130},{256,131},... | collective-permute-start | bytes 6152 | tf_op jit(solution)/shard_map/ppermute | solution.py:25
  571.9 21.7 %collective-permute-start.38 = (f32[8,1,64]{2,1,0:T(1,128)S(1)}, f32[8,1,64]{2,1,0:T(1,128)S(1)}, u32[]{:S(2)}, u32[]{:S(2)}) collective-permute-start(f32[8,1,64]{2,1,0:T(1,128)S(1)} %get-tuple-element.121), channel_id=1, source_target_pairs={{1,0},{2,1},{3,2},{128,3},{129,128},{130,129},{131,130},{256,131},... | collective-permute-start | bytes 6152 | tf_op jit(solution)/shard_map/ppermute | solution.py:25
  598.6 21.7 %collective-permute-start.42 = (f32[16,1,128]{2,1,0:T(1,128)S(1)}, f32[16,1,128]{2,1,0:T(1,128)S(1)}, u32[]{:S(2)}, u32[]{:S(2)}) collective-permute-start(f32[16,1,128]{2,1,0:T(1,128)S(1)} %get-tuple-element.89), channel_id=1, source_target_pairs={{1,0},{2,1},{3,2},{128,3},{129,128},{130,129},{131,130},{256,131},... | collective-permute-start | bytes 24584 | tf_op jit(solution)/shard_map/ppermute | solution.py:25
  677.7 41.3 %collective-permute-start.54 = (f32[16,1,128]{2,1,0:T(1,128)S(1)}, f32[16,1,128]{2,1,0:T(1,128)S(1)}, u32[]{:S(2)}, u32[]{:S(2)}) collective-permute-start(f32[16,1,128]{2,1,0:T(1,128)S(1)} %get-tuple-element.77), channel_id=1, source_target_pairs={{1,0},{2,1},{3,2},{128,3},{129,128},{130,129},{131,130},{256,131},... | collective-permute-start | bytes 24584 | tf_op jit(solution)/shard_map/ppermute | solution.py:25
  679.6 39.4 %collective-permute-start.55 = (f32[16,1,128]{2,1,0:T(1,128)S(1)}, f32[16,1,128]{2,1,0:T(1,128)S(1)}, u32[]{:S(2)}, u32[]{:S(2)}) collective-permute-start(f32[16,1,128]{2,1,0:T(1,128)S(1)} %get-tuple-element.76), channel_id=1, source_target_pairs={{0,1},{1,2},{2,3},{3,128},{128,129},{129,130},{130,131},{131,256},... | collective-permute-start | bytes 24584 | tf_op jit(solution)/shard_map/ppermute | solution.py:24
  694.1 24.9 %collective-permute-start.52 = (f32[1,8,128]{2,1,0:T(8,128)S(1)}, f32[1,8,128]{2,1,0:T(8,128)S(1)}, u32[]{:S(2)}, u32[]{:S(2)}) collective-permute-start(f32[1,8,128]{2,1,0:T(8,128)S(1)} %get-tuple-element.75), channel_id=1, source_target_pairs={{4,0},{8,4},{12,8},{16,12},{20,16},{24,20},{28,24},{32,28},{36,32}... | collective-permute-start | bytes 12296 | tf_op jit(solution)/shard_map/ppermute | solution.py:25
  696.0 23.0 %collective-permute-start.53 = (f32[1,8,128]{2,1,0:T(8,128)S(1)}, f32[1,8,128]{2,1,0:T(8,128)S(1)}, u32[]{:S(2)}, u32[]{:S(2)}) collective-permute-start(f32[1,8,128]{2,1,0:T(8,128)S(1)} %get-tuple-element.74), channel_id=1, source_target_pairs={{0,4},{4,8},{8,12},{12,16},{16,20},{20,24},{24,28},{28,32},{32,36}... | collective-permute-start | bytes 12296 | tf_op jit(solution)/shard_map/ppermute | solution.py:24
  714.7 158.0 %all-to-all-start.4 = ((f32[16,1,16384]{2,1,0:T(1,128)}), f32[16,1,16384]{2,1,0:T(1,128)S(1)}, u32[]{:S(2)}, u32[]{:S(2)}) async-start(f32[16,1,16384]{2,1,0:T(1,128)} %reshape.358), calls=%async_computation.4 | async-start | bytes 2097152 | tf_op jit(solution)/shard_map/all_to_all | solution.py:170
  719.4 24.1 %collective-permute-start.58 = (f32[16,1,128]{2,1,0:T(1,128)S(1)}, f32[16,1,128]{2,1,0:T(1,128)S(1)}, u32[]{:S(2)}, u32[]{:S(2)}) collective-permute-start(f32[16,1,128]{2,1,0:T(1,128)S(1)} %get-tuple-element.73), channel_id=1, source_target_pairs={{1,0},{2,1},{3,2},{128,3},{129,128},{130,129},{131,130},{256,131},... | collective-permute-start | bytes 24584 | tf_op jit(solution)/shard_map/ppermute | solution.py:25
  791.2 22.4 %collective-permute-start.66 = (f32[8,1,64]{2,1,0:T(1,128)S(1)}, f32[8,1,64]{2,1,0:T(1,128)S(1)}, u32[]{:S(2)}, u32[]{:S(2)}) collective-permute-start(f32[8,1,64]{2,1,0:T(1,128)S(1)} %get-tuple-element.113), channel_id=1, source_target_pairs={{1,0},{2,1},{3,2},{128,3},{129,128},{130,129},{131,130},{256,131},... | collective-permute-start | bytes 6152 | tf_op jit(solution)/shard_map/ppermute | solution.py:25
  820.2 21.7 %collective-permute-start.70 = (f32[4,1,32]{2,0,1:T(4,128)S(1)}, f32[4,1,32]{2,0,1:T(4,128)S(1)}, u32[]{:S(2)}, u32[]{:S(2)}) collective-permute-start(f32[4,1,32]{2,0,1:T(4,128)S(1)} %get-tuple-element.145), channel_id=1, source_target_pairs={{1,0},{2,1},{3,2},{128,3},{129,128},{130,129},{131,130},{256,131},... | collective-permute-start | bytes 1544 | tf_op jit(solution)/shard_map/ppermute | solution.py:25
  904.2 141.9 %all-to-all-start.5 = ((f32[32,1,8192]{2,1,0:T(1,128)}), f32[32,1,8192]{2,1,0:T(1,128)S(1)}, u32[]{:S(2)}, u32[]{:S(2)}) async-start(f32[32,1,8192]{2,1,0:T(1,128)} %reshape.360), calls=%async_computation.5 | async-start | bytes 2097152 | tf_op jit(solution)/shard_map/all_to_all | solution.py:176
  911.1 22.6 %collective-permute-start.78 = (f32[4,1,32]{2,0,1:T(4,128)S(1)}, f32[4,1,32]{2,0,1:T(4,128)S(1)}, u32[]{:S(2)}, u32[]{:S(2)}) collective-permute-start(f32[4,1,32]{2,0,1:T(4,128)S(1)} %get-tuple-element.137), channel_id=1, source_target_pairs={{1,0},{2,1},{3,2},{128,3},{129,128},{130,129},{131,130},{256,131},... | collective-permute-start | bytes 1544 | tf_op jit(solution)/shard_map/ppermute | solution.py:25
  966.1 21.7 %collective-permute-start.86 = (f32[8,1,64]{2,1,0:T(1,128)S(1)}, f32[8,1,64]{2,1,0:T(1,128)S(1)}, u32[]{:S(2)}, u32[]{:S(2)}) collective-permute-start(f32[8,1,64]{2,1,0:T(1,128)S(1)} %get-tuple-element.105), channel_id=1, source_target_pairs={{1,0},{2,1},{3,2},{128,3},{129,128},{130,129},{131,130},{256,131},... | collective-permute-start | bytes 6152 | tf_op jit(solution)/shard_map/ppermute | solution.py:25
  (83 other events, 1139.3 us)
